TPU v7x, 32 devices: a 4x4x1 block of a 4x4x8 slice. The times are simulated.
32 devices in a mesh: rep: 1 (over z), dp: 32 (over x, y, core).
Axes of the slice: x: 4, y: 4, z: 1, core: 2. Of those that a mesh axis runs over, the one named last changes fastest.
The devices are a block of a 4x4x8 slice.
Arguments:
- g_w_gate: bfloat16 [32, 2, 1024, 3200], P(('rep', 'dp'))
- g_w_up: bfloat16 [32, 2, 1024, 3200], P(('rep', 'dp'))
- g_w_down: bfloat16 [32, 2, 3200, 1024], P(('rep', 'dp'))
- w_gate: bfloat16 [2, 1024, 3200], replicated
- w_up: bfloat16 [2, 1024, 3200], replicated
- w_down: bfloat16 [2, 3200, 1024], replicated
- m_w_gate: float32 [2, 1024, 3200], P(None, 'dp')
- m_w_up: float32 [2, 1024, 3200], P(None, 'dp')
- m_w_down: float32 [2, 3200, 1024], P(None, 'dp')
- v_w_gate: float32 [2, 1024, 3200], P(None, 'dp')
- v_w_up: float32 [2, 1024, 3200], P(None, 'dp')
- v_w_down: float32 [2, 3200, 1024], P(None, 'dp')
Outputs:
- output 1: bfloat16 [2, 1024, 3200], P('rep')
- output 2: bfloat16 [2, 1024, 3200], P('rep')
- output 3: bfloat16 [2, 3200, 1024], P('rep')
- output 4: float32 [2, 1024, 3200], P('rep', 'dp')
- output 5: float32 [2, 1024, 3200], P('rep', 'dp')
- output 6: float32 [2, 3200, 1024], P('rep', 'dp')
- output 7: float32 [2, 1024, 3200], P('rep', 'dp')
- output 8: float32 [2, 1024, 3200], P('rep', 'dp')
- output 9: float32 [2, 3200, 1024], P('rep', 'dp')
All inputs are finite; a program needn't handle non-finite values.
Results may differ from a plain program's by a relative error of at most 0.022.
Values are sent between devices in bfloat16 or wider.
A program may use at most 768 MiB of HBM per device.

v0:
```python
import jax
import jax.numpy as jnp
from jax import lax
from jax.sharding import PartitionSpec as P


def adamw(w, m, v, g):
    m = 0.9 * m + 0.1 * g
    v = 0.95 * v + 0.05 * g * g
    step = m * lax.rsqrt(v + 1e-8) + 0.1 * w
    return (w - 0.02 * step).astype(jnp.bfloat16), m, v


def solution(mesh):
    def step(*arrays):
        terms, weights, m, v = (arrays[i : i + 3] for i in (0, 3, 6, 9))
        gradients = [lax.psum_scatter(t[0], "dp", scatter_dimension=1, tiled=True).astype(jnp.float32) for t in terms]
        me = lax.axis_index("dp")
        own = [lax.dynamic_slice_in_dim(w, me * one.shape[1], one.shape[1], 1).astype(jnp.float32) for w, one in zip(weights, m, strict=True)]
        new = [adamw(w, m, v, g) for w, m, v, g in zip(own, m, v, gradients, strict=True)]
        whole = [lax.all_gather(one[0], "dp", axis=1, tiled=True) for one in new]
        return (*whole, *(one[1] for one in new), *(one[2] for one in new))

    all_of, cut = P(None, None, None), P(None, "dp", None)
    return jax.shard_map(
        step,
        mesh=mesh,
        in_specs=(P(("rep", "dp"), None, None, None),) * 3 + (all_of,) * 3 + (cut,) * 6,
        out_specs=(P("rep", None, None),) * 3 + (P("rep", "dp", None),) * 6,
        check_vma=False,
    )
```

profile of v0, /device:TPU:97, one launch (start us, length us, event | category | flops | bytes accessed | tf_op | source)
XLA Modules:
  0.0 568.9 jit_solution(819550753651997038)
XLA Ops:
  7.2 0.1 all-reduce.3.cloned.1.call-start
  7.3 24.6 %copy.30 = bf16[1,2,3200,1024]{3,1,2,0:T(2,128)(2,1)} copy(bf16[1,2,3200,1024]{3,2,1,0:T(8,128)(2,1)} %param.14) | data formatting | bytes 26214400 | tf_op args[2]
  31.8 0.1 all-reduce.3.cloned.1.call-update
  31.9 0.1 reduce-scatter.5.cloned.1.call-start
  32.0 0.0 copy-start.1
  32.0 0.0 copy-start.2
  32.0 0.0 copy-start.3
  32.0 0.7 reduce-scatter.5.cloned.1.call-update
  32.7 0.1 reduce-scatter.3.cloned.1.call-start
  32.8 0.7 reduce-scatter.3.cloned.1.call-update
  33.5 0.1 all-gather.8.cloned.1.call-start
  33.6 1.1 constant_dynamic-slice_fusion
  34.7 124.5 %all-reduce.3.cloned.1.call-done = bf16[2,3200,1024]{2,0,1:T(2,128)(2,1)} async-done(((bf16[2,3200,1024]{2,0,1:T(2,128)(2,1)}), bf16[2,3200,1024]{2,0,1:T(2,128)(2,1)}) %all-reduce.3.cloned.1.call-update) | async-done | bytes 13107216
  159.2 0.0 copy-done.1
  159.2 0.0 copy-done.2
  159.2 5.1 fusion.14
  164.3 0.1 all-gather.8.cloned.1.call-update
  164.4 0.1 all-gather.6.cloned.1.call-start
  164.4 94.2 %reduce-scatter.5.cloned.1.call-done = bf16[2,32,3200]{2,1,0:T(8,128)(2,1)} async-done(((bf16[2,1024,3200]{2,1,0:T(8,128)(2,1)}), bf16[2,32,3200]{2,1,0:T(8,128)(2,1)}) %reduce-scatter.5.cloned.1.call-update) | async-done | bytes 409616 | tf_op jit(solution)/shard_map/reduce_scatter | solution.py:17
  258.6 0.0 copy-done.3
  258.6 2.9 fusion.6
  261.5 0.1 all-gather.6.cloned.1.call-update
  261.5 0.1 all-gather.4.cloned.1.call-start
  261.6 97.9 %reduce-scatter.3.cloned.1.call-done = bf16[2,32,3200]{2,1,0:T(8,128)(2,1)} async-done(((bf16[2,1024,3200]{2,1,0:T(8,128)(2,1)}), bf16[2,32,3200]{2,1,0:T(8,128)(2,1)}) %reduce-scatter.3.cloned.1.call-update) | async-done | bytes 409616 | tf_op jit(solution)/shard_map/reduce_scatter | solution.py:17
  359.5 3.1 fusion.2
  362.7 0.1 all-gather.4.cloned.1.call-update
  362.7 59.6 %all-gather.8.cloned.1.call-done = bf16[2,3200,1024]{2,0,1:T(2,128)(2,1)} async-done(((bf16[2,100,1024]{2,0,1:T(2,128)(2,1)}), bf16[2,3200,1024]{2,0,1:T(2,128)(2,1)}) %all-gather.8.cloned.1.call-update) | async-done | bytes 13107216 | tf_op jit(solution)/shard_map/all_gather | solution.py:21
  422.3 12.9 %copy.26 = bf16[2,3200,1024]{2,1,0:T(8,128)(2,1)} copy(bf16[2,3200,1024]{2,0,1:T(2,128)(2,1)} %all-gather.8.cloned.1.call-done) | data formatting | bytes 26214400
  435.3 47.7 %all-gather.6.cloned.1.call-done = bf16[2,1024,3200]{2,1,0:T(8,128)(2,1)} async-done(((bf16[2,32,3200]{2,1,0:T(8,128)(2,1)}), bf16[2,1024,3200]{2,1,0:T(8,128)(2,1)}) %all-gather.6.cloned.1.call-update) | async-done | bytes 13107216 | tf_op jit(solution)/shard_map/all_gather | solution.py:21
  483.0 60.7 %all-gather.4.cloned.1.call-done = bf16[2,1024,3200]{2,1,0:T(8,128)(2,1)} async-done(((bf16[2,32,3200]{2,1,0:T(8,128)(2,1)}), bf16[2,1024,3200]{2,1,0:T(8,128)(2,1)}) %all-gather.4.cloned.1.call-update) | async-done | bytes 13107216 | tf_op jit(solution)/shard_map/all_gather | solution.py:21
  543.7 0.0 copy-start
  543.7 11.4 %copy.34 = bf16[2,1024,3200]{2,1,0:T(8,128)(2,1)} copy(bf16[2,1024,3200]{2,1,0:T(8,128)(2,1)} %all-gather.4.cloned.1.call-done) | data formatting | bytes 26214400
  555.0 2.0 copy-done
  557.1 4.9 copy.35
Async XLA Ops:
  7.2 152.0 %all-reduce.3.cloned.1.call-start = ((), (), s32[]{:S(2)}) async-start(), calls=%async_computation.7 | async-start | bytes 26214400
  31.9 226.7 %reduce-scatter.5.cloned.1.call-start = ((), (), s32[]{:S(2)}) async-start(), calls=%async_computation.4 | async-start | bytes 13516800 | tf_op jit(solution)/shard_map/reduce_scatter | solution.py:17
  32.0 127.2 %copy-start.1 = (f32[2,100,1024]{2,0,1:T(2,128)S(1)}, f32[2,100,1024]{2,0,1:T(2,128)}, u32[]{:S(2)}) copy-start(f32[2,100,1024]{2,0,1:T(2,128)} %param.23) | copy-start | bytes 2457604
  32.0 127.2 %copy-start.2 = (f32[2,100,1024]{2,0,1:T(2,128)S(1)}, f32[2,100,1024]{2,0,1:T(2,128)}, u32[]{:S(2)}) copy-start(f32[2,100,1024]{2,0,1:T(2,128)} %param.20) | copy-start | bytes 2457604
  32.0 226.6 %copy-start.3 = (f32[2,32,3200]{2,1,0:T(8,128)S(1)}, f32[2,32,3200]{2,1,0:T(8,128)}, u32[]{:S(2)}) copy-start(f32[2,32,3200]{2,1,0:T(8,128)} %param.22) | copy-start | bytes 2457604
  32.7 326.8 %reduce-scatter.3.cloned.1.call-start = ((), (), s32[]{:S(2)}) async-start(), calls=%async_computation.2 | async-start | bytes 13516800 | tf_op jit(solution)/shard_map/reduce_scatter | solution.py:17
  33.5 388.8 %all-gather.8.cloned.1.call-start = ((), (), s32[]{:S(2)}) async-start(), calls=%async_computation.6 | async-start | bytes 13516800 | tf_op jit(solution)/shard_map/all_gather | solution.py:21
  164.4 318.6 %all-gather.6.cloned.1.call-start = ((), (), s32[]{:S(2)}) async-start(), calls=%async_computation.5 | async-start | bytes 13516800 | tf_op jit(solution)/shard_map/all_gather | solution.py:21
  261.5 282.1 %all-gather.4.cloned.1.call-start = ((), (), s32[]{:S(2)}) async-start(), calls=%async_computation.3 | async-start | bytes 13516800 | tf_op jit(solution)/shard_map/all_gather | solution.py:21
  543.7 13.4 %copy-start = (bf16[2,1024,3200]{2,1,0:T(8,128)(2,1)S(1)}, bf16[2,1024,3200]{2,1,0:T(8,128)(2,1)}, u32[]{:S(2)}) copy-start(bf16[2,1024,3200]{2,1,0:T(8,128)(2,1)} %all-gather.6.cloned.1.call-done) | copy-start | bytes 39321604
Sparse Core Ops, SparseCore 0:
  32.0 127.1 all-reduce.2
  162.9 95.6 reduce-scatter.4
  262.3 97.1 reduce-scatter.2
  362.0 60.2 all-gather.7
  424.9 58.0 all-gather.5
  485.5 58.0 all-gather.3
where the time goes:
time: 569 us
  waiting for transfers between devices  486 us (85%)
  local copies, waits for them, and re-layouts  57 us (10%)
  between operations  14.2 us (2%)
  other arithmetic  11.1 us (2%)
    reduce_scatter x2, waiting for transfers between devices, step(): lax.psum_scatter(t[0], 'dp', scatter_dimension=1, tiled=True)  192 us
    all_gather x3, waiting for transfers between devices, step(): whole = [lax.all_gather(one[0], 'dp', axis=1, tiled=True) for one in new]  168 us
    unnamed x7, waiting for transfers between devices  126 us
    unnamed x12, local copies, waits for them, and re-layouts  55.9 us
  transfers between devices with their start and end apart: 6, of which 6 were waited for; matrix products, arithmetic and copies ran while one was open for 4% of the time, Pallas kernels for 0%

commit v1 on v0

v1 whole, which is shorter than its diff:
```python
import functools
import math

import jax
import jax.numpy as jnp
from jax import lax
from jax.experimental import pallas as pl
from jax.experimental.pallas import tpu as pltpu
from jax.sharding import PartitionSpec as P

MESH = pl.DeviceIdType.MESH
F32, BF16 = jnp.float32, jnp.bfloat16
SLOTS = 16
AHEAD = 12


def adamw(w, m, v, g):
    m = 0.9 * m + 0.1 * g
    v = 0.95 * v + 0.05 * g * g
    step = m * lax.rsqrt(v + 1e-8) + 0.1 * w
    return w - 0.02 * step, m, v


def step_kernel(n, *refs):
    g, w, m, v = (refs[i : i + 3] for i in (0, 3, 6, 9))
    ow, om, ov = (refs[i : i + 3] for i in (12, 15, 18))
    own, wsl = refs[21:24], refs[24:27]
    xg, xw, yw, zw, tmp = refs[27:32]
    ring_send, ring_recv, core_send, core_recv, all_recv, own_sem, in_sem, x_sems, ready = refs[32:]

    side = math.isqrt(n // 2)
    last = side - 1
    chips = side * side
    rows = m[0].shape[1]
    half = rows // 2
    tall = 2 * m[2].shape[1]
    low = m[2].shape[1]
    off = low // 8 * 8
    frame = tall - off
    shift = low - off
    quarter = ow[2].shape[2] // 4
    unit = 3 * half
    total = 4 * chips

    me = lax.axis_index("dp")
    k = lax.rem(me, 2)
    chip = lax.div(me, 2)
    x, y = lax.div(chip, side), lax.rem(chip, side)
    partner = me + 1 - 2 * k

    def wrap(z):
        return lax.rem(z + 2 * side, side)

    class Colour:
        def __init__(self, q):
            self.q = q
            self.l = a = lax.div(q, 2)
            self.h = lax.rem(q, 2)
            self.dir = 1 - 2 * self.h
            self.p1, self.p2 = x + a * (y - x), y + a * (x - y)
            self.a = a

        def chip(self, u, v):
            u, v = wrap(u), wrap(v)
            return (u + self.a * (v - u)) * side + v + self.a * (u - v)

        def next1(self):
            return self.chip(self.p1 + self.dir, self.p2) * 2 + k

        def next2(self):
            return self.chip(self.p1, self.p2 + self.dir) * 2 + k

        def back(self, i, j):
            return self.chip(self.p1 - self.dir * i, self.p2 - self.dir * j)

    def place(p, at, core, col):
        if p < 2:
            return (col.l, pl.ds(pl.multiple_of(at * (2 * rows) + core * rows + col.h * half, half), half))
        return (
            col.l,
            pl.ds(pl.multiple_of(at * tall, 8), tall),
            pl.ds(pl.multiple_of(core * (2 * quarter) + col.h * quarter, quarter), quarter),
        )

    def remote(src, dst, send, recv, device):
        return pltpu.make_async_remote_copy(
            src_ref=src, dst_ref=dst, send_sem=send, recv_sem=recv, device_id={"dp": device}, device_id_type=MESH
        )

    def wait_bytes(sem, chunks):
        part = ow[0].at[0, pl.ds(0, chunks * unit)]
        pltpu.make_async_copy(part, part, sem).wait()

    def wait_piece(p, sem):
        part = ow[0].at[0, pl.ds(0, half)]
        pltpu.make_async_copy(part, part, sem).wait()

    def chunk(t):
        s, j, col = lax.div(t, 4 * side), lax.rem(lax.div(t, 4), side), Colour(lax.rem(t, 4))
        return col, col.back(1 + s, 1 + j)

    def to_partner(t):
        col, at = chunk(t)
        for p in range(3):
            i = place(p, at, 1 - k, col)
            remote(g[p].at[(0, *i)], ow[p].at[i], core_send.at[col.q], core_recv.at[t], partner).start()

    def load_own(t):
        col, at = chunk(t)
        slot = lax.rem(t, SLOTS)
        for p in range(3):
            pltpu.make_async_copy(g[p].at[(0, *place(p, at, k, col))], own[p].at[slot], own_sem.at[slot]).start()

    def wait_own(slot):
        part = own[0].at[pl.ds(0, 3)]
        pltpu.make_async_copy(part, part, own_sem.at[slot]).wait()

    def each(count, body):
        lax.fori_loop(0, count, lambda i, c: (body(i), c)[1], 0)

    peers = [
        (wrap(x + dx) * side + wrap(y + dy)) * 2 + k for dx, dy in ((1, 0), (-1, 0), (0, 1), (0, -1))
    ] + [partner]
    barrier = pltpu.get_barrier_semaphore()
    for peer in peers:
        pl.semaphore_signal(barrier, inc=1, device_id={"dp": peer}, device_id_type=MESH)
    each(SLOTS, load_own)
    pl.semaphore_wait(barrier, len(peers))
    each(AHEAD, to_partner)

    loads = []
    for p in range(3):
        if p < 2:
            part = w[p].at[:, pl.ds(pl.multiple_of(me * rows, rows), rows)]
        else:
            part = w[p].at[:, pl.ds(pl.multiple_of(chip * tall + off * k, 8), frame)]
        loads.append(pltpu.make_async_copy(part, wsl[p], in_sem.at[p]))
        loads.append(pltpu.make_async_copy(m[p], om[p], in_sem.at[3 + p]))
        loads.append(pltpu.make_async_copy(v[p], ov[p], in_sem.at[6 + p]))
    for copy in loads:
        copy.start()

    def reduce_chunk(t, s, j, col, second):
        at = col.back(1 + s, 1 + j)
        slot = lax.rem(t, SLOTS)
        wait_bytes(core_recv.at[t], 1)
        wait_own(slot)
        first = not isinstance(s, int) or s > 0
        for p in range(3):
            i = place(p, at, k, col)
            so_far = ow[p][i].astype(F32) + own[p][slot].astype(F32)
            if first:
                r = (s - 1) * side + j
                wait_piece(p, ring_recv.at[col.q, r, p])
                so_far += ow[p][place(p, r, 1 - k, col)].astype(F32)
            if second and j > 0:
                r = last * side + j - 1
                wait_piece(p, ring_recv.at[col.q, r, p])
                so_far += ow[p][place(p, r, 1 - k, col)].astype(F32)
            ow[p][i] = so_far.astype(BF16)
        if second and j == last:
            return
        for p in range(3):
            i = place(p, at, k, col)
            r = s * side + j
            there = ow[p].at[place(p, r, 1 - k, col)]
            device = col.next2() if second else col.next1()
            remote(ow[p].at[i], there, ring_send.at[col.q], ring_recv.at[col.q, r, p], device).start()

    def refill(t):
        @pl.when(t + SLOTS < total)
        def _():
            load_own(t + SLOTS)

        @pl.when(t + AHEAD < total)
        def _():
            to_partner(t + AHEAD)

    def round_zero(i):
        reduce_chunk(i, 0, lax.div(i, 4), Colour(lax.rem(i, 4)), False)
        refill(i)

    def round_more(i):
        t = i + 4 * side
        reduce_chunk(t, lax.div(t, 4 * side), lax.rem(lax.div(t, 4), side), Colour(lax.rem(t, 4)), False)
        refill(t)

    each(4 * side, round_zero)
    each(4 * side * (last - 1), round_more)
    for j in range(side):

        def round_last(q):
            t = (last * side + j) * 4 + q
            reduce_chunk(t, last, j, Colour(q), True)
            refill(t)

        each(4, round_last)

    def swap(q):
        col = Colour(q)
        part = ow[2].at[
            col.l,
            pl.ds(pl.multiple_of(chip * tall + off * (1 - k), 8), frame),
            pl.ds(pl.multiple_of(k * (2 * quarter) + col.h * quarter, quarter), quarter),
        ]
        return remote(part, xg.at[q], x_sems.at[0, q], x_sems.at[1, q], partner)

    each(4, lambda q: swap(q).start())

    for q in range(4):
        wait_bytes(ring_send.at[q], chips - 1)
        wait_bytes(core_send.at[q], chips)
    for peer in peers:
        pl.semaphore_signal(ready, inc=1, device_id={"dp": peer}, device_id_type=MESH)
    for copy in loads:
        copy.wait()

    def wide_step(q):
        col = Colour(q)
        here = pl.ds(pl.multiple_of(col.h * half, half), half)
        for p in range(2):
            i = place(p, chip, k, col)
            new, new_m, new_v = adamw(
                wsl[p][col.l, here].astype(F32), om[p][col.l, here], ov[p][col.l, here], ow[p][i].astype(F32)
            )
            ow[p][i] = new.astype(BF16)
            om[p][col.l, here] = new_m
            ov[p][col.l, here] = new_v

    def spread(q, i, j, pieces):
        col = Colour(q)
        at = col.back(i, j)
        for p in pieces:
            if i + j > 0:
                wait_piece(p, ring_recv.at[q, i * side + j, p])
            part = ow[p].at[place(p, at, k, col)]
            if i == 0 and j < last:
                remote(part, part, ring_send.at[q], ring_recv.at[q, j + 1, p], col.next2()).start()
            if i < last:
                remote(part, part, ring_send.at[q], ring_recv.at[q, (i + 1) * side + j, p], col.next1()).start()
            remote(part, part, core_send.at[q], all_recv.at[q], partner).start()

    each(4, wide_step)
    pl.semaphore_wait(ready, len(peers))
    each(4, lambda q: spread(q, 0, 0, (0, 1)))

    def give(q):
        return remote(zw.at[q], xw.at[q], x_sems.at[2, q], x_sems.at[3, q], partner)

    def tall_step(q):
        col = Colour(q)
        swap(q).wait()
        for core in range(2):

            @pl.when(k == core)
            def _():
                for mine in (True, False):
                    side_of = core if mine else 1 - core
                    cols = pl.ds(pl.multiple_of(side_of * 2 * quarter + col.h * quarter, quarter), quarter)
                    if mine:
                        grad = ow[2][col.l, pl.ds(pl.multiple_of(chip * tall + off * core, 8), frame), cols]
                    else:
                        grad = xg[q]
                    at = slice(shift * core, shift * core + low)
                    new, new_m, new_v = adamw(
                        wsl[2][col.l, :, cols].astype(F32)[at],
                        om[2][col.l, :, cols],
                        ov[2][col.l, :, cols],
                        grad.astype(F32)[at],
                    )
                    om[2][col.l, :, cols] = new_m
                    ov[2][col.l, :, cols] = new_v
                    tmp[at, :] = new
                    (yw if mine else zw)[q] = tmp[...]

        give(q).start()

    tmp[...] = jnp.zeros_like(tmp)
    each(4, tall_step)

    def join(q):
        col = Colour(q)
        give(q).wait()
        cols = pl.ds(pl.multiple_of(k * 2 * quarter + col.h * quarter, quarter), quarter)
        base = chip * tall

        def put(start, value):
            ow[2][col.l, pl.ds(pl.multiple_of(base + start, 8), value.shape[0]), cols] = value.astype(BF16)

        for core in range(2):

            @pl.when(k == core)
            def _():
                top, bottom = (yw, xw) if core == 0 else (xw, yw)
                put(0, top[q, 0:off, :])
                row = lax.broadcasted_iota(jnp.int32, (8, quarter), 0)
                put(off, jnp.where(row < shift, top[q, off : off + 8, :], bottom[q, 0:8, :]))
                put(off + 8, bottom[q, 8:frame, :])

        spread(q, 0, 0, (2,))

    each(4, join)

    order = [(0, 1), (1, 0), (0, 2), (1, 1), (0, 3), (1, 2), (1, 3)]
    order += [(i, j) for i in range(2, side) for j in range(side)]
    order = [(i, j) for i, j in order if i < side and j < side]
    for i, j in order:
        each(4, lambda q, i=i, j=j: spread(q, i, j, (0, 1, 2)))
    for q in range(4):
        wait_bytes(ring_send.at[q], chips - 1)
        wait_bytes(core_send.at[q], chips)
        wait_bytes(all_recv.at[q], chips)


def drain_kernel(count, *refs):
    sem = refs[-1]
    copies = [pltpu.make_async_copy(refs[i], refs[count + i], sem.at[i]) for i in range(count)]
    for copy in copies:
        copy.start()
    for copy in copies:
        copy.wait()


def drain(arrays):
    count = len(arrays)
    return list(
        pl.pallas_call(
            functools.partial(drain_kernel, count),
            out_shape=[jax.ShapeDtypeStruct(a.shape, a.dtype) for a in arrays],
            in_specs=[pl.BlockSpec(memory_space=pltpu.VMEM)] * count,
            out_specs=[pl.BlockSpec(memory_space=pl.ANY)] * count,
            scratch_shapes=[pltpu.SemaphoreType.DMA((count,))],
            compiler_params=pltpu.CompilerParams(vmem_limit_bytes=1 << 20),
        )(*arrays)
    )


def solution(mesh):
    n = mesh.shape["dp"]

    def step(*arrays):
        g, w, m, v = (arrays[i : i + 3] for i in (0, 3, 6, 9))
        rows, wide = m[0].shape[1:]
        low, narrow = m[2].shape[1:]
        side = math.isqrt(n // 2)
        half, quarter = rows // 2, narrow // 4
        frame = 2 * low - low // 8 * 8
        assert half * wide == 2 * low * quarter and side * side * 2 == n and low % 8
        dma, regular = pltpu.SemaphoreType.DMA, pltpu.SemaphoreType.REGULAR
        outs = pl.pallas_call(
            functools.partial(step_kernel, n),
            out_shape=[pltpu.VMEM(a.shape, a.dtype) for a in (*w, *m, *v)],
            in_specs=[pl.BlockSpec(memory_space=pltpu.HBM)] * 12,
            out_specs=[pl.BlockSpec(memory_space=pltpu.VMEM)] * 9,
            scratch_shapes=[
                pltpu.VMEM((SLOTS, half, wide), BF16),
                pltpu.VMEM((SLOTS, half, wide), BF16),
                pltpu.VMEM((SLOTS, 2 * low, quarter), BF16),
                pltpu.VMEM((2, rows, wide), BF16),
                pltpu.VMEM((2, rows, wide), BF16),
                pltpu.VMEM((2, frame, narrow), BF16),
                pltpu.VMEM((4, frame, quarter), BF16),
                pltpu.VMEM((4, frame, quarter), F32),
                pltpu.VMEM((4, frame, quarter), F32),
                pltpu.VMEM((4, frame, quarter), F32),
                pltpu.VMEM((frame, quarter), F32),
                dma((4,)),
                dma((4, side * side, 3)),
                dma((4,)),
                dma((4 * side * side,)),
                dma((4,)),
                dma((SLOTS,)),
                dma((9,)),
                dma((4, 4)),
                regular,
            ],
            compiler_params=pltpu.CompilerParams(
                collective_id=0, has_side_effects=True, vmem_limit_bytes=14 << 20
            ),
        )(*g, *w, *m, *v)
        outs = [*drain(outs[0:1]), *drain(outs[1:2]), *drain(outs[2:3]), *drain(outs[3:])]
        return tuple(outs)

    all_of, cut = P(None, None, None), P(None, "dp", None)
    return jax.shard_map(
        step,
        mesh=mesh,
        in_specs=(P(("rep", "dp"), None, None, None),) * 3 + (all_of,) * 3 + (cut,) * 6,
        out_specs=(P("rep", None, None),) * 3 + (P("rep", "dp", None),) * 6,
        check_vma=False,
    )
```

time: 569 us -> 258 us (0.45)
  waiting for transfers between devices: 486 us -> 0 us
  Pallas kernels: 0 us -> 240 us
  local copies, waits for them, and re-layouts: 57 us -> 17.3 us
  between operations: 14.2 us -> 0.68 us
  other arithmetic: 11.1 us -> 0 us
    pallas_call x0 -> x5, Pallas kernels: none -> 240 us  [the longest x1 223 us: step(): pl.pallas_call(functools.partial(step_kernel, n), out_shape=[pltpu.VMEM(a...]
    reduce_scatter x2 -> x0, waiting for transfers between devices: 192 us -> none  [step(): lax.psum_scatter(t[0], 'dp', scatter_dimension=1, tiled=True)]
    all_gather x3 -> x0, waiting for transfers between devices: 168 us -> none  [step(): whole = [lax.all_gather(one[0], 'dp', axis=1, tiled=True) for one in new]]
    unnamed x7 -> x0, waiting for transfers between devices: 126 us -> none
    unnamed x12 -> x8, local copies, waits for them, and re-layouts: 55.9 us -> 17.3 us
    convert_element_type x3 -> x0, other arithmetic: 11.1 us -> none  [adamw(): return ((w - 0.02 * step).astype(jnp.bfloat16), m, v)]
  transfers between devices with their start and end apart: 6 -> 0, of which waited for: 6 -> 0; matrix products, arithmetic and copies ran while one was open for 4% -> 0% of each run, Pallas kernels for 0% -> 0%
where the time goes in v1:
time: 258 us
  Pallas kernels  240 us (93%)
  local copies, waits for them, and re-layouts  17.3 us (7%)
    pallas_call x1, Pallas kernels, step(): pl.pallas_call(functools.partial(step_kernel, n), out_shape=[pltpu.VMEM(a...  223 us
    unnamed x8, local copies, waits for them, and re-layouts  17.3 us
    pallas_call x4, Pallas kernels, drain(): pl.pallas_call(functools.partial(drain_kernel, count), out_shape=[jax.Sha...  16.6 us

profile of v1, /device:TPU:97, one launch (start us, length us, event | category | flops | bytes accessed | tf_op | source)
XLA Modules:
  0.0 258.1 jit_solution(4114640342434550764)
XLA Ops:
  0.6 2.3 copy.21.refs_8_
  3.0 2.3 copy.22.refs_11_
  5.3 223.5 %shard_map.187 = (bf16[2,1024,3200]{2,1,0:T(8,128)(2,1)S(1)}, bf16[2,1024,3200]{2,1,0:T(8,128)(2,1)S(1)}, bf16[2,3200,1024]{2,1,0:T(8,128)(2,1)S(1)}, f32[2,32,3...) custom-call(bf16[1,2,1024,3200]{3,2,1,0:T(8,128)(2,1)} %refs_0_.1, ...), custom_call_target="tpu_custom_call" | custom-call | tf_op jit(solution)/shard_map/pallas_call | solution.py:350
  228.7 0.0 copy-start
  228.7 4.9 %copy-done = bf16[2,1024,3200]{2,1,0:T(8,128)(2,1)} copy-done((bf16[2,1024,3200]{2,1,0:T(8,128)(2,1)}, bf16[2,1024,3200]{2,1,0:T(8,128)(2,1)S(1)}, u32[]{:S(2)}) %copy-start) | copy-done | bytes 13107224
  233.7 1.8 shard_map.191
  235.4 1.5 copy.23
  237.0 1.5 copy.24
  238.5 0.0 copy-start.1
  238.5 4.7 %copy-done.1 = bf16[2,1024,3200]{2,1,0:T(8,128)(2,1)S(1)} copy-done((bf16[2,1024,3200]{2,1,0:T(8,128)(2,1)S(1)}, bf16[2,1024,3200]{2,1,0:T(8,128)(2,1)}, u32[]{:S(2)}) %copy-start.1) | copy-done | bytes 13107224
  243.2 5.0 %shard_map.188 = bf16[2,1024,3200]{2,1,0:T(8,128)(2,1)} custom-call(bf16[2,1024,3200]{2,1,0:T(8,128)(2,1)S(1)} %copy-done.1), custom_call_target="tpu_custom_call" | custom-call | tf_op jit(solution)/shard_map/pallas_call | solution.py:327
  248.2 5.0 %shard_map.189 = bf16[2,1024,3200]{2,1,0:T(8,128)(2,1)} custom-call(bf16[2,1024,3200]{2,1,0:T(8,128)(2,1)S(1)} %get-tuple-element.25.refs_0_), custom_call_target="tpu_custom_call" | custom-call | tf_op jit(solution)/shard_map/pallas_call | solution.py:327
  253.1 5.0 %shard_map.190 = bf16[2,3200,1024]{2,1,0:T(8,128)(2,1)} custom-call(bf16[2,3200,1024]{2,1,0:T(8,128)(2,1)S(1)} %get-tuple-element.26.refs_0_), custom_call_target="tpu_custom_call" | custom-call | tf_op jit(solution)/shard_map/pallas_call | solution.py:327
Async XLA Ops:
  228.7 5.0 %copy-start = (bf16[2,1024,3200]{2,1,0:T(8,128)(2,1)}, bf16[2,1024,3200]{2,1,0:T(8,128)(2,1)S(1)}, u32[]{:S(2)}) copy-start(bf16[2,1024,3200]{2,1,0:T(8,128)(2,1)S(1)} %get-tuple-element.24.refs_0_) | copy-start | bytes 39321604
  238.5 4.7 %copy-start.1 = (bf16[2,1024,3200]{2,1,0:T(8,128)(2,1)S(1)}, bf16[2,1024,3200]{2,1,0:T(8,128)(2,1)}, u32[]{:S(2)}) copy-start(bf16[2,1024,3200]{2,1,0:T(8,128)(2,1)} %copy-done) | copy-start | bytes 39321604

commit v2 on v1

v2 whole, which is shorter than its diff:
```python
import functools
import math

import jax
import jax.numpy as jnp
from jax import lax
from jax.experimental import pallas as pl
from jax.experimental.pallas import tpu as pltpu
from jax.sharding import PartitionSpec as P

MESH = pl.DeviceIdType.MESH
F32, BF16 = jnp.float32, jnp.bfloat16
SLOTS = 16
PARTS = 8
STAGES = (2, 0, 1)


def adamw(w, m, v, g):
    m = 0.9 * m + 0.1 * g
    v = 0.95 * v + 0.05 * g * g
    step = m * lax.rsqrt(v + 1e-8) + 0.1 * w
    return w - 0.02 * step, m, v


def step_kernel(n, *refs):
    g, w, m, v = (refs[i : i + 3] for i in (0, 3, 6, 9))
    ow, om, ov = (refs[i : i + 3] for i in (12, 15, 18))
    own, wsl = refs[21:24], refs[24:27]
    xg, xw, yw, zw, tmp = refs[27:32]
    ring_send, ring_recv, core_send, core_recv, all_recv, own_sem, in_sem, x_sems, ready = refs[32:]

    side = math.isqrt(n // 2)
    last = side - 1
    chips = side * side
    rows = m[0].shape[1]
    half = rows // 2
    low = m[2].shape[0]
    tall = 2 * low
    off = low // 8 * 8
    frame = tall - off
    shift = low - off
    quarter = ow[2].shape[2] // 4
    total = 4 * chips
    ahead = 4 * side

    me = lax.axis_index("dp")
    k = lax.rem(me, 2)
    chip = lax.div(me, 2)
    x, y = lax.div(chip, side), lax.rem(chip, side)
    partner = me + 1 - 2 * k

    def wrap(z):
        return lax.rem(z + 2 * side, side)

    class Colour:
        def __init__(self, q):
            self.q = q
            self.l = a = lax.div(q, 2)
            self.h = lax.rem(q, 2)
            self.dir = 1 - 2 * self.h
            self.p1, self.p2 = x + a * (y - x), y + a * (x - y)
            self.a = a

        def chip(self, u, v):
            u, v = wrap(u), wrap(v)
            return (u + self.a * (v - u)) * side + v + self.a * (u - v)

        def next1(self):
            return self.chip(self.p1 + self.dir, self.p2) * 2 + k

        def next2(self):
            return self.chip(self.p1, self.p2 + self.dir) * 2 + k

        def back(self, i, j):
            return self.chip(self.p1 - self.dir * i, self.p2 - self.dir * j)

    def place(p, at, core, col):
        if p < 2:
            return (col.l, pl.ds(pl.multiple_of(at * (2 * rows) + core * rows + col.h * half, half), half))
        return (
            col.l,
            pl.ds(pl.multiple_of(at * tall, 8), tall),
            pl.ds(pl.multiple_of(core * (2 * quarter) + col.h * quarter, quarter), quarter),
        )

    def remote(src, dst, send, recv, device):
        return pltpu.make_async_remote_copy(
            src_ref=src, dst_ref=dst, send_sem=send, recv_sem=recv, device_id={"dp": device}, device_id_type=MESH
        )

    def wait_pieces(sem, count):
        part = ow[0].at[0, pl.ds(0, count * half)]
        pltpu.make_async_copy(part, part, sem).wait()

    def split(t):
        s, j, col = lax.div(t, 4 * side), lax.rem(lax.div(t, 4), side), Colour(lax.rem(t, 4))
        return col, col.back(1 + s, 1 + j)

    def to_partner(p, t):
        col, at = split(t)
        i = place(p, at, 1 - k, col)
        remote(g[p].at[(0, *i)], ow[p].at[i], core_send.at[p, col.q], core_recv.at[p, t], partner).start()

    def load_own(p, t):
        col, at = split(t)
        slot = lax.rem(t, SLOTS)
        pltpu.make_async_copy(g[p].at[(0, *place(p, at, k, col))], own[p].at[slot], own_sem.at[p, slot]).start()

    def each(count, body):
        lax.fori_loop(0, count, lambda i, c: (body(i), c)[1], 0)

    peers = [
        (wrap(x + dx) * side + wrap(y + dy)) * 2 + k for dx, dy in ((1, 0), (-1, 0), (0, 1), (0, -1))
    ] + [partner]
    barrier = pltpu.get_barrier_semaphore()
    for peer in peers:
        pl.semaphore_signal(barrier, inc=1, device_id={"dp": peer}, device_id_type=MESH)
    for p in STAGES:
        each(SLOTS, functools.partial(load_own, p))
    pl.semaphore_wait(barrier, len(peers))
    each(ahead, functools.partial(to_partner, STAGES[0]))

    loads = []
    for p in range(3):
        if p < 2:
            part = w[p].at[:, pl.ds(pl.multiple_of(me * rows, rows), rows)]
        else:
            part = w[p].at[:, pl.ds(pl.multiple_of(chip * tall + off * k, 8), frame)]
        loads.append(pltpu.make_async_copy(part, wsl[p], in_sem.at[p]))
        loads.append(pltpu.make_async_copy(m[p], om[p], in_sem.at[3 + p]))
        loads.append(pltpu.make_async_copy(v[p], ov[p], in_sem.at[6 + p]))
    for copy in loads:
        copy.start()

    def reduce(p, s, j, q):
        col = Colour(q)
        at = col.back(1 + s, 1 + j)
        t = (s * side + j) * 4 + q
        slot = lax.rem(t, SLOTS)
        second = isinstance(s, int) and s == last
        i = place(p, at, k, col)
        wait_pieces(core_recv.at[p, t], 1)
        wait_pieces(own_sem.at[p, slot], 1)
        so_far = ow[p][i].astype(F32) + own[p][slot].astype(F32)
        came = []
        if not isinstance(s, int) or s > 0:
            came.append((s - 1) * side + j)
        if second and j > 0:
            came.append(last * side + j - 1)
        for r in came:
            wait_pieces(ring_recv.at[p, q, r], 1)
            so_far += ow[p][place(p, r, 1 - k, col)].astype(F32)
        ow[p][i] = so_far.astype(BF16)
        if not (second and j == last):
            r = s * side + j
            there = ow[p].at[place(p, r, 1 - k, col)]
            device = col.next2() if second else col.next1()
            remote(ow[p].at[i], there, ring_send.at[p, q], ring_recv.at[p, q, r], device).start()

        @pl.when(t + SLOTS < total)
        def _():
            load_own(p, t + SLOTS)

        @pl.when(t + ahead < total)
        def _():
            to_partner(p, t + ahead)

        if p != STAGES[-1]:

            @pl.when((t >= total - 2 * ahead) & (t < total - ahead))
            def _():
                to_partner(STAGES[STAGES.index(p) + 1], t + 2 * ahead - total)

    def round_of(p, s):
        each(4 * side, lambda i: reduce(p, s, lax.div(i, 4), lax.rem(i, 4)))

    def few(p, s, j):
        each(4, lambda q: reduce(p, s, j, q))

    def let_in(p):
        for q in range(4):
            wait_pieces(ring_send.at[p, q], chips - 1)
            wait_pieces(core_send.at[p, q], chips)
        for peer in peers:
            pl.semaphore_signal(ready.at[p], inc=1, device_id={"dp": peer}, device_id_type=MESH)

    def spread(p, i, j, q):
        col = Colour(q)
        at = col.back(i, j)
        if i + j > 0:
            wait_pieces(ring_recv.at[p, q, i * side + j], 1)
        part = ow[p].at[place(p, at, k, col)]
        if i == 0 and j < last:
            remote(part, part, ring_send.at[p, q], ring_recv.at[p, q, j + 1], col.next2()).start()
        if i < last:
            remote(part, part, ring_send.at[p, q], ring_recv.at[p, q, (i + 1) * side + j], col.next1()).start()
        remote(part, part, core_send.at[p, q], all_recv.at[p, q], partner).start()

    def wide_step(p, q):
        col = Colour(q)
        here = pl.ds(pl.multiple_of(col.h * half, half), half)
        i = place(p, chip, k, col)
        new, new_m, new_v = adamw(
            wsl[p][col.l, here].astype(F32), om[p][col.l, here], ov[p][col.l, here], ow[p][i].astype(F32)
        )
        ow[p][i] = new.astype(BF16)
        om[p][col.l, here] = new_m
        ov[p][col.l, here] = new_v

    def swap(q):
        col = Colour(q)
        part = ow[2].at[
            col.l,
            pl.ds(pl.multiple_of(chip * tall + off * (1 - k), 8), frame),
            pl.ds(pl.multiple_of(k * (2 * quarter) + col.h * quarter, quarter), quarter),
        ]
        return remote(part, xg.at[q], x_sems.at[0, q], x_sems.at[1, q], partner)

    def give(q):
        return remote(zw.at[q], xw.at[q], x_sems.at[2, q], x_sems.at[3, q], partner)

    def tall_step(q):
        l, h = q // 2, q % 2
        swap(q).wait()
        for core in range(2):

            @pl.when(k == core)
            def _():
                for mine in (True, False):
                    side_of = core if mine else 1 - core
                    cols = pl.ds(side_of * 2 * quarter + h * quarter, quarter)
                    if mine:
                        grad = ow[2][l, pl.ds(pl.multiple_of(chip * tall + off * core, 8), frame), cols]
                    else:
                        grad = xg[q]
                    at = slice(shift * core, shift * core + low)
                    new, new_m, new_v = adamw(
                        wsl[2][l, :, cols].astype(F32)[at],
                        om[2][:, l, cols],
                        ov[2][:, l, cols],
                        grad.astype(F32)[at],
                    )
                    om[2][:, l, cols] = new_m
                    ov[2][:, l, cols] = new_v
                    tmp[at, :] = new
                    (yw if mine else zw)[q] = tmp[...]

        give(q).start()

    def join(q):
        col = Colour(q)
        give(q).wait()
        cols = pl.ds(pl.multiple_of(k * 2 * quarter + col.h * quarter, quarter), quarter)
        base = chip * tall

        def put(start, value):
            ow[2][col.l, pl.ds(pl.multiple_of(base + start, 8), value.shape[0]), cols] = value.astype(BF16)

        for core in range(2):

            @pl.when(k == core)
            def _():
                top, bottom = (yw, xw) if core == 0 else (xw, yw)
                put(0, top[q, 0:off, :])
                row = lax.broadcasted_iota(jnp.int32, (8, quarter), 0)
                put(off, jnp.where(row < shift, top[q, off : off + 8, :], bottom[q, 0:8, :]))
                put(off + 8, bottom[q, 8:frame, :])

    first, middle, final = STAGES
    assert first == 2
    tmp[...] = jnp.zeros_like(tmp)

    round_of(first, 0)
    each(last - 1, lambda s: round_of(first, s + 1))
    for j in range(side):
        few(middle, 0, j)
        few(first, last, j)
    each(4, lambda q: swap(q).start())
    round_of(middle, 1)
    let_in(first)
    for copy in loads:
        copy.wait()
    for q in range(4):
        tall_step(q)
    each(last - 2, lambda s: round_of(middle, s + 2))
    each(4, join)
    for j in range(side):
        few(final, 0, j)
        few(middle, last, j)
    round_of(final, 1)
    let_in(middle)
    each(4, lambda q: wide_step(middle, q))
    each(last - 2, lambda s: round_of(final, s + 2))
    few(final, last, 0)
    pl.semaphore_wait(ready.at[first], len(peers))
    each(4, lambda q: spread(first, 0, 0, q))
    few(final, last, 1)
    pl.semaphore_wait(ready.at[middle], len(peers))
    each(4, lambda q: spread(middle, 0, 0, q))
    for j in range(2, side):
        few(final, last, j)
    let_in(final)
    each(4, lambda q: spread(first, 0, 1, q))
    each(4, lambda q: wide_step(final, q))
    pl.semaphore_wait(ready.at[final], len(peers))
    each(4, lambda q: spread(final, 0, 0, q))

    order = [(0, 1), (1, 0), (0, 2), (1, 1), (0, 3), (1, 2), (1, 3)]
    order += [(i, j) for i in range(2, side) for j in range(side)]
    order = [(i, j) for i, j in order if i < side and j < side]
    for i, j in order:
        for p in STAGES:
            if (p, i, j) != (first, 0, 1):
                each(4, lambda q, p=p, i=i, j=j: spread(p, i, j, q))
    for p in range(3):
        for q in range(4):
            wait_pieces(ring_send.at[p, q], chips - 1)
            wait_pieces(core_send.at[p, q], chips)
            wait_pieces(all_recv.at[p, q], chips)


def drain_kernel(count, *refs):
    sem = refs[-1]
    copies = []
    for i in range(count):
        here, there = refs[i], refs[count + i]
        parts = PARTS if here.shape[1] % (8 * PARTS) == 0 else 1
        size = here.shape[1] // parts
        for a in range(here.shape[0] if parts > 1 else 1):
            for b in range(parts):
                at = (a, pl.ds(b * size, size)) if parts > 1 else (slice(None),)
                copies.append(pltpu.make_async_copy(here.at[at], there.at[at], sem.at[len(copies)]))
    for copy in copies:
        copy.start()
    for copy in copies:
        copy.wait()


def drain(arrays):
    count = len(arrays)
    return list(
        pl.pallas_call(
            functools.partial(drain_kernel, count),
            out_shape=[jax.ShapeDtypeStruct(a.shape, a.dtype) for a in arrays],
            in_specs=[pl.BlockSpec(memory_space=pltpu.VMEM)] * count,
            out_specs=[pl.BlockSpec(memory_space=pl.ANY)] * count,
            scratch_shapes=[pltpu.SemaphoreType.DMA((2 * PARTS * count,))],
            compiler_params=pltpu.CompilerParams(vmem_limit_bytes=1 << 20),
        )(*arrays)
    )


def solution(mesh):
    n = mesh.shape["dp"]

    def step(*arrays):
        g, w, m, v = (list(arrays[i : i + 3]) for i in (0, 3, 6, 9))
        m[2], v[2] = m[2].swapaxes(0, 1), v[2].swapaxes(0, 1)
        rows, wide = m[0].shape[1:]
        low, _, narrow = m[2].shape
        side = math.isqrt(n // 2)
        half, quarter = rows // 2, narrow // 4
        frame = 2 * low - low // 8 * 8
        assert half * wide == 2 * low * quarter and side * side * 2 == n and low % 8
        dma, regular = pltpu.SemaphoreType.DMA, pltpu.SemaphoreType.REGULAR
        outs = pl.pallas_call(
            functools.partial(step_kernel, n),
            out_shape=[pltpu.VMEM(a.shape, a.dtype) for a in (*w, *m, *v)],
            in_specs=[pl.BlockSpec(memory_space=pltpu.HBM)] * 12,
            out_specs=[pl.BlockSpec(memory_space=pltpu.VMEM)] * 9,
            scratch_shapes=[
                pltpu.VMEM((SLOTS, half, wide), BF16),
                pltpu.VMEM((SLOTS, half, wide), BF16),
                pltpu.VMEM((SLOTS, 2 * low, quarter), BF16),
                pltpu.VMEM((2, rows, wide), BF16),
                pltpu.VMEM((2, rows, wide), BF16),
                pltpu.VMEM((2, frame, narrow), BF16),
                pltpu.VMEM((4, frame, quarter), BF16),
                pltpu.VMEM((4, frame, quarter), F32),
                pltpu.VMEM((4, frame, quarter), F32),
                pltpu.VMEM((4, frame, quarter), F32),
                pltpu.VMEM((frame, quarter), F32),
                dma((3, 4)),
                dma((3, 4, side * side)),
                dma((3, 4)),
                dma((3, 4 * side * side)),
                dma((3, 4)),
                dma((3, SLOTS)),
                dma((9,)),
                dma((4, 4)),
                regular((3,)),
            ],
            compiler_params=pltpu.CompilerParams(
                collective_id=0, has_side_effects=True, vmem_limit_bytes=14 << 20
            ),
        )(*g, *w, *m, *v)
        outs = [*drain(outs[0:1]), *drain(outs[1:2]), *drain(outs[2:3]), *drain(outs[3:])]
        for i in (5, 8):
            outs[i] = outs[i].swapaxes(0, 1)
        return tuple(outs)

    all_of, cut = P(None, None, None), P(None, "dp", None)
    return jax.shard_map(
        step,
        mesh=mesh,
        in_specs=(P(("rep", "dp"), None, None, None),) * 3 + (all_of,) * 3 + (cut,) * 6,
        out_specs=(P("rep", None, None),) * 3 + (P("rep", "dp", None),) * 6,
        check_vma=False,
    )
```

time: 258 us -> 240 us (0.930)
  local copies, waits for them, and re-layouts: 17.3 us -> 0 us
    unnamed x8 -> x0, local copies, waits for them, and re-layouts: 17.3 us -> none
where the time goes in v2:
time: 240 us
  Pallas kernels  239 us (100%)
    pallas_call x1, Pallas kernels, step(): pl.pallas_call(functools.partial(step_kernel, n), out_shape=[pltpu.VMEM(a...  221 us
    pallas_call x4, Pallas kernels, drain(): pl.pallas_call(functools.partial(drain_kernel, count), out_shape=[jax.Sha...  17.7 us

profile of v2, /device:TPU:97, one launch (start us, length us, event | category | flops | bytes accessed | tf_op | source)
XLA Modules:
  0.0 239.7 jit_solution(17201919262636181739)
XLA Ops:
  0.6 221.2 %shard_map.187 = (bf16[2,1024,3200]{2,1,0:T(8,128)(2,1)S(1)}, bf16[2,1024,3200]{2,1,0:T(8,128)(2,1)S(1)}, bf16[2,3200,1024]{2,1,0:T(8,128)(2,1)S(1)}, f32[2,32,3...) custom-call(bf16[1,2,1024,3200]{3,2,1,0:T(8,128)(2,1)} %refs_0_.1, ...), custom_call_target="tpu_custom_call" | custom-call | tf_op jit(solution)/shard_map/pallas_call | solution.py:366
  221.8 4.9 %shard_map.188 = bf16[2,1024,3200]{2,1,0:T(8,128)(2,1)} custom-call(bf16[2,1024,3200]{2,1,0:T(8,128)(2,1)S(1)} %get-tuple-element.24.refs_0_), custom_call_target="tpu_custom_call" | custom-call | tf_op jit(solution)/shard_map/pallas_call | solution.py:342
  226.7 3.1 %shard_map.191 = (f32[2,32,3200]{2,1,0:T(8,128)}, f32[2,32,3200]{2,1,0:T(8,128)}, f32[100,2,1024]{2,1,0:T(2,128)}, f32[2,32,3200]{2,1,0:T(8,128)}, f32[2,32,3200]{2,1,0:T(8,128)}, /*index=5*/f32[100,2,1024]{2,1,0:T(2,128)}) custom-call(f32[2,32,3200]{2,1,0:T(8,128)S(1)} %get-tuple-element.27.refs_0_, f32[2,32,3200]{2,1,0:T(8,128)S(1)} %get-tuple-element.28.refs_1_, ...), custom_call_target="tpu_custom_call" | custom-call | tf_op jit(solution)/shard_map/pallas_call | solution.py:342
  229.8 4.9 %shard_map.189 = bf16[2,1024,3200]{2,1,0:T(8,128)(2,1)} custom-call(bf16[2,1024,3200]{2,1,0:T(8,128)(2,1)S(1)} %get-tuple-element.25.refs_0_), custom_call_target="tpu_custom_call" | custom-call | tf_op jit(solution)/shard_map/pallas_call | solution.py:342
  234.7 4.9 %shard_map.190 = bf16[2,3200,1024]{2,1,0:T(8,128)(2,1)} custom-call(bf16[2,3200,1024]{2,1,0:T(8,128)(2,1)S(1)} %get-tuple-element.26.refs_0_), custom_call_target="tpu_custom_call" | custom-call | tf_op jit(solution)/shard_map/pallas_call | solution.py:342

commit v3 on v2

--- a/solution.py
+++ b/solution.py
@@ -171,9 +171,6 @@
             def _():
                 to_partner(STAGES[STAGES.index(p) + 1], t + 2 * ahead - total)
 
-    def round_of(p, s):
-        each(4 * side, lambda i: reduce(p, s, lax.div(i, 4), lax.rem(i, 4)))
-
     def few(p, s, j):
         each(4, lambda q: reduce(p, s, j, q))
 
@@ -270,48 +267,73 @@
     assert first == 2
     tmp[...] = jnp.zeros_like(tmp)
 
-    round_of(first, 0)
-    each(last - 1, lambda s: round_of(first, s + 1))
-    for j in range(side):
-        few(middle, 0, j)
-        few(first, last, j)
-    each(4, lambda q: swap(q).start())
-    round_of(middle, 1)
-    let_in(first)
-    for copy in loads:
-        copy.wait()
-    for q in range(4):
-        tall_step(q)
-    each(last - 2, lambda s: round_of(middle, s + 2))
-    each(4, join)
-    for j in range(side):
-        few(final, 0, j)
-        few(middle, last, j)
-    round_of(final, 1)
-    let_in(middle)
-    each(4, lambda q: wide_step(middle, q))
-    each(last - 2, lambda s: round_of(final, s + 2))
-    few(final, last, 0)
-    pl.semaphore_wait(ready.at[first], len(peers))
-    each(4, lambda q: spread(first, 0, 0, q))
-    few(final, last, 1)
-    pl.semaphore_wait(ready.at[middle], len(peers))
-    each(4, lambda q: spread(middle, 0, 0, q))
-    for j in range(2, side):
-        few(final, last, j)
-    let_in(final)
-    each(4, lambda q: spread(first, 0, 1, q))
-    each(4, lambda q: wide_step(final, q))
-    pl.semaphore_wait(ready.at[final], len(peers))
-    each(4, lambda q: spread(final, 0, 0, q))
-
-    order = [(0, 1), (1, 0), (0, 2), (1, 1), (0, 3), (1, 2), (1, 3)]
+    def inner(p):
+        return [functools.partial(few, p, s, j) for s in range(last) for j in range(side)]
+
+    def weave(p, before, extra):
+        for at, run in enumerate(inner(p)):
+            if at % last == 0:
+                few(before, last, at // last)
+            run()
+            for more in extra.get(at, ()):
+                more()
+
+    def some(body, *qs):
+        def run():
+            for q in qs:
+                body(q)
+
+        return run
+
+    order = [(0, 0), (0, 1), (1, 0), (0, 2), (1, 1), (0, 3), (1, 2), (1, 3)]
     order += [(i, j) for i in range(2, side) for j in range(side)]
     order = [(i, j) for i, j in order if i < side and j < side]
-    for i, j in order:
-        for p in STAGES:
-            if (p, i, j) != (first, 0, 1):
-                each(4, lambda q, p=p, i=i, j=j: spread(p, i, j, q))
+    left = {p: list(order) for p in STAGES}
+
+    def hand_on(p):
+        if left[p]:
+            i, j = left[p].pop(0)
+            if i + j == 0:
+                pl.semaphore_wait(ready.at[p], len(peers))
+            each(4, lambda q: spread(p, i, j, q))
+
+    for run in inner(first):
+        run()
+    end = last * side - 1
+    weave(middle, first, {end - 2: [lambda: each(4, lambda q: swap(q).start())]})
+    weave(
+        final,
+        middle,
+        {
+            0: [functools.partial(let_in, first)] + [copy.wait for copy in loads] + [some(tall_step, 0)],
+            2: [some(tall_step, 1)],
+            3: [some(tall_step, 2)],
+            5: [some(tall_step, 3)],
+            7: [some(join, 0, 1)],
+            8: [some(join, 2, 3)],
+            end - 1: [functools.partial(let_in, middle), some(functools.partial(wide_step, middle), 0, 1)],
+            end: [some(functools.partial(wide_step, middle), 2, 3)],
+        },
+    )
+    few(final, last, 0)
+    hand_on(first)
+    hand_on(middle)
+    few(final, last, 1)
+    hand_on(first)
+    hand_on(first)
+    few(final, last, 2)
+    hand_on(middle)
+    hand_on(first)
+    for j in range(3, side):
+        few(final, last, j)
+    hand_on(middle)
+    let_in(final)
+    for q in range(4):
+        wide_step(final, q)
+        hand_on(STAGES[q % 2])
+    while any(left.values()):
+        for p in (final, first, middle):
+            hand_on(p)
     for p in range(3):
         for q in range(4):
             wait_pieces(ring_send.at[p, q], chips - 1)

time: 240 us -> 233 us (0.971)
  Pallas kernels: 239 us -> 232 us
    pallas_call x1, Pallas kernels: 221 us -> 214 us  [step(): pl.pallas_call(functools.partial(step_kernel, n), out_shape=[pltpu.VMEM(a...]
where the time goes in v3:
time: 233 us
  Pallas kernels  232 us (100%)
    pallas_call x1, Pallas kernels, step(): pl.pallas_call(functools.partial(step_kernel, n), out_shape=[pltpu.VMEM(a...  214 us
    pallas_call x4, Pallas kernels, drain(): pl.pallas_call(functools.partial(drain_kernel, count), out_shape=[jax.Sha...  17.7 us

profile of v3, /device:TPU:97, one launch (start us, length us, event | category | flops | bytes accessed | tf_op | source)
XLA Modules:
  0.0 232.9 jit_solution(4517622238637430985)
XLA Ops:
  0.6 214.3 %shard_map.187 = (bf16[2,1024,3200]{2,1,0:T(8,128)(2,1)S(1)}, bf16[2,1024,3200]{2,1,0:T(8,128)(2,1)S(1)}, bf16[2,3200,1024]{2,1,0:T(8,128)(2,1)S(1)}, f32[2,32,3...) custom-call(bf16[1,2,1024,3200]{3,2,1,0:T(8,128)(2,1)} %refs_0_.1, ...), custom_call_target="tpu_custom_call" | custom-call | tf_op jit(solution)/shard_map/pallas_call | solution.py:388
  215.0 4.9 %shard_map.188 = bf16[2,1024,3200]{2,1,0:T(8,128)(2,1)} custom-call(bf16[2,1024,3200]{2,1,0:T(8,128)(2,1)S(1)} %get-tuple-element.24.refs_0_), custom_call_target="tpu_custom_call" | custom-call | tf_op jit(solution)/shard_map/pallas_call | solution.py:364
  219.9 3.1 %shard_map.191 = (f32[2,32,3200]{2,1,0:T(8,128)}, f32[2,32,3200]{2,1,0:T(8,128)}, f32[100,2,1024]{2,1,0:T(2,128)}, f32[2,32,3200]{2,1,0:T(8,128)}, f32[2,32,3200]{2,1,0:T(8,128)}, /*index=5*/f32[100,2,1024]{2,1,0:T(2,128)}) custom-call(f32[2,32,3200]{2,1,0:T(8,128)S(1)} %get-tuple-element.27.refs_0_, f32[2,32,3200]{2,1,0:T(8,128)S(1)} %get-tuple-element.28.refs_1_, ...), custom_call_target="tpu_custom_call" | custom-call | tf_op jit(solution)/shard_map/pallas_call | solution.py:364
  223.0 4.9 %shard_map.189 = bf16[2,1024,3200]{2,1,0:T(8,128)(2,1)} custom-call(bf16[2,1024,3200]{2,1,0:T(8,128)(2,1)S(1)} %get-tuple-element.25.refs_0_), custom_call_target="tpu_custom_call" | custom-call | tf_op jit(solution)/shard_map/pallas_call | solution.py:364
  227.9 4.9 %shard_map.190 = bf16[2,3200,1024]{2,1,0:T(8,128)(2,1)} custom-call(bf16[2,3200,1024]{2,1,0:T(8,128)(2,1)S(1)} %get-tuple-element.26.refs_0_), custom_call_target="tpu_custom_call" | custom-call | tf_op jit(solution)/shard_map/pallas_call | solution.py:364

commit v4 on v0

v4 whole, which is shorter than its diff:
```python
import functools
import math

import jax
import jax.numpy as jnp
from jax import lax
from jax.experimental import pallas as pl
from jax.experimental.pallas import tpu as pltpu
from jax.sharding import PartitionSpec as P

MESH = pl.DeviceIdType.MESH
F32, BF16 = jnp.float32, jnp.bfloat16
SLOTS = 16
PARTS = 8
WIDE, TALL = 0, 1


def adamw(w, m, v, g):
    m = 0.9 * m + 0.1 * g
    v = 0.95 * v + 0.05 * g * g
    step = m * lax.rsqrt(v + 1e-8) + 0.1 * w
    return w - 0.02 * step, m, v


def step_kernel(n, *refs):
    g, w, m, v = (refs[i : i + 3] for i in (0, 3, 6, 9))
    weights, (om, om_tall, ov, ov_tall) = refs[12:14], refs[14:18]
    own, wsl, wsl_tall = refs[18:20], refs[20], refs[21]
    xg, xw, yw, zw, tmp = refs[22:27]
    ring_send, ring_recv, core_send, core_recv, all_recv, own_sem, in_sem, x_sems, ready = refs[27:]

    side = math.isqrt(n // 2)
    last = side - 1
    chips = side * side
    rows = m[0].shape[1]
    low = m[2].shape[0]
    tall = 2 * low
    off = low // 8 * 8
    frame = tall - off
    shift = low - off
    quarter = weights[TALL].shape[2] // 4
    total = 4 * chips
    ahead = 4 * side
    piece_rows = (rows, rows // 2)

    me = lax.axis_index("dp")
    k = lax.rem(me, 2)
    chip = lax.div(me, 2)
    x, y = lax.div(chip, side), lax.rem(chip, side)
    partner = me + 1 - 2 * k

    def wrap(z):
        return lax.rem(z + 2 * side, side)

    class Colour:
        def __init__(self, q):
            self.q = q
            self.a, self.b = lax.div(q, 2), lax.rem(q, 2)
            self.dir = 1 - 2 * self.b
            self.p1, self.p2 = x + self.a * (y - x), y + self.a * (x - y)

        def chip(self, u, v):
            u, v = wrap(u), wrap(v)
            return (u + self.a * (v - u)) * side + v + self.a * (u - v)

        def next1(self):
            return self.chip(self.p1 + self.dir, self.p2) * 2 + k

        def next2(self):
            return self.chip(self.p1, self.p2 + self.dir) * 2 + k

        def back(self, i, j):
            return self.chip(self.p1 - self.dir * i, self.p2 - self.dir * j)

    def within(p, at, core, col):
        if p == WIDE:
            return (pl.ds(pl.multiple_of((at * 2 + core) * rows, rows), rows),)
        return (
            pl.ds(pl.multiple_of(at * tall, 8), tall),
            pl.ds(pl.multiple_of(core * (2 * quarter) + col.b * quarter, quarter), quarter),
        )

    def place(p, at, core, col):
        return (col.q if p == WIDE else col.a, *within(p, at, core, col))

    def from_terms(p, at, core, col, use):
        part = within(p, at, core, col)
        if p == TALL:
            use(g[2].at[(0, col.a, *part)])
            return
        for a in range(2):

            @pl.when(col.a == a)
            def _():
                use(g[a].at[(0, col.b, *part)])

    def remote(src, dst, send, recv, device):
        return pltpu.make_async_remote_copy(
            src_ref=src, dst_ref=dst, send_sem=send, recv_sem=recv, device_id={"dp": device}, device_id_type=MESH
        )

    def wait_pieces(p, sem, count):
        part = weights[WIDE].at[0, pl.ds(0, count * piece_rows[p])]
        pltpu.make_async_copy(part, part, sem).wait()

    def split(t):
        s, j, col = lax.div(t, 4 * side), lax.rem(lax.div(t, 4), side), Colour(lax.rem(t, 4))
        return col, col.back(1 + s, 1 + j)

    def to_partner(p, t):
        col, at = split(t)
        there = weights[p].at[place(p, at, 1 - k, col)]
        send, recv = core_send.at[p, col.q], core_recv.at[p, t]
        from_terms(p, at, 1 - k, col, lambda term: remote(term, there, send, recv, partner).start())

    def load_own(p, t):
        col, at = split(t)
        slot = lax.rem(t, SLOTS)
        here, sem = own[p].at[slot], own_sem.at[p, slot]
        from_terms(p, at, k, col, lambda term: pltpu.make_async_copy(term, here, sem).start())

    def each(count, body):
        lax.fori_loop(0, count, lambda i, c: (body(i), c)[1], 0)

    peers = [
        (wrap(x + dx) * side + wrap(y + dy)) * 2 + k for dx, dy in ((1, 0), (-1, 0), (0, 1), (0, -1))
    ] + [partner]
    barrier = pltpu.get_barrier_semaphore()
    for peer in peers:
        pl.semaphore_signal(barrier, inc=1, device_id={"dp": peer}, device_id_type=MESH)
    each(SLOTS, functools.partial(load_own, TALL))
    pl.semaphore_wait(barrier, len(peers))
    each(ahead, functools.partial(to_partner, TALL))
    each(SLOTS, functools.partial(load_own, WIDE))

    here = pl.ds(pl.multiple_of(me * rows, rows), rows)
    rim = pl.ds(pl.multiple_of(chip * tall + off * k, 8), frame)
    pairs = [(w[2].at[:, rim], wsl_tall), (m[2], om_tall), (v[2], ov_tall)]
    for a in range(2):
        half = pl.ds(2 * a, 2)
        pairs += [(w[a].at[:, here], wsl.at[half]), (m[a], om.at[half]), (v[a], ov.at[half])]
    loads = [pltpu.make_async_copy(src, dst, in_sem.at[i]) for i, (src, dst) in enumerate(pairs)]
    for copy in loads:
        copy.start()

    def reduce(p, s, j, q):
        col = Colour(q)
        at = col.back(1 + s, 1 + j)
        t = (s * side + j) * 4 + q
        slot = lax.rem(t, SLOTS)
        i = place(p, at, k, col)
        out = weights[p]
        wait_pieces(p, core_recv.at[p, t], 1)
        wait_pieces(p, own_sem.at[p, slot], 1)
        so_far = out[i].astype(F32) + own[p][slot].astype(F32)
        came = [(s - 1) * side + j] if s > 0 else []
        if s == last and j > 0:
            came.append(last * side + j - 1)
        for r in came:
            wait_pieces(p, ring_recv.at[p, q, r], 1)
            so_far += out[place(p, r, 1 - k, col)].astype(F32)
        out[i] = so_far.astype(BF16)
        if s < last or j < last:
            r = s * side + j
            there = out.at[place(p, r, 1 - k, col)]
            device = col.next2() if s == last else col.next1()
            remote(out.at[i], there, ring_send.at[p, q], ring_recv.at[p, q, r], device).start()
        if (s * side + j) * 4 + SLOTS < total:
            load_own(p, t + SLOTS)
        if (s * side + j) * 4 + ahead < total:
            to_partner(p, t + ahead)
        if p == TALL and s == last - 1:
            to_partner(WIDE, t + 2 * ahead - total)

    def few(p, s, j):
        each(4, lambda q: reduce(p, s, j, q))

    def let_in(p):
        for q in range(4):
            wait_pieces(p, ring_send.at[p, q], chips - 1)
            wait_pieces(p, core_send.at[p, q], chips)
        for peer in peers:
            pl.semaphore_signal(ready.at[p], inc=1, device_id={"dp": peer}, device_id_type=MESH)

    def spread(p, i, j, q):
        col = Colour(q)
        at = col.back(i, j)
        if i + j > 0:
            wait_pieces(p, ring_recv.at[p, q, i * side + j], 1)
        part = weights[p].at[place(p, at, k, col)]
        if i == 0 and j < last:
            remote(part, part, ring_send.at[p, q], ring_recv.at[p, q, j + 1], col.next2()).start()
        if i < last:
            remote(part, part, ring_send.at[p, q], ring_recv.at[p, q, (i + 1) * side + j], col.next1()).start()
        remote(part, part, core_send.at[p, q], all_recv.at[p, q], partner).start()

    def wide_step(q):
        i = place(WIDE, chip, k, Colour(q))
        new, new_m, new_v = adamw(wsl[q].astype(F32), om[q], ov[q], weights[WIDE][i].astype(F32))
        weights[WIDE][i] = new.astype(BF16)
        om[q] = new_m
        ov[q] = new_v

    def swap(q):
        col = Colour(q)
        part = weights[TALL].at[
            col.a,
            pl.ds(pl.multiple_of(chip * tall + off * (1 - k), 8), frame),
            pl.ds(pl.multiple_of(k * (2 * quarter) + col.b * quarter, quarter), quarter),
        ]
        return remote(part, xg.at[q], x_sems.at[0, q], x_sems.at[1, q], partner)

    def give(q):
        return remote(zw.at[q], xw.at[q], x_sems.at[2, q], x_sems.at[3, q], partner)

    def tall_step(q):
        a, b = q // 2, q % 2
        swap(q).wait()
        for core in range(2):

            @pl.when(k == core)
            def _():
                for mine in (True, False):
                    side_of = core if mine else 1 - core
                    cols = pl.ds(side_of * 2 * quarter + b * quarter, quarter)
                    if mine:
                        grad = weights[TALL][a, pl.ds(pl.multiple_of(chip * tall + off * core, 8), frame), cols]
                    else:
                        grad = xg[q]
                    at = slice(shift * core, shift * core + low)
                    new, new_m, new_v = adamw(
                        wsl_tall[a, :, cols].astype(F32)[at],
                        om_tall[:, a, cols],
                        ov_tall[:, a, cols],
                        grad.astype(F32)[at],
                    )
                    om_tall[:, a, cols] = new_m
                    ov_tall[:, a, cols] = new_v
                    tmp[at, :] = new
                    (yw if mine else zw)[q] = tmp[...]

        give(q).start()

    def join(q):
        col = Colour(q)
        give(q).wait()
        cols = pl.ds(pl.multiple_of(k * 2 * quarter + col.b * quarter, quarter), quarter)
        base = chip * tall

        def put(start, value):
            part = pl.ds(pl.multiple_of(base + start, 8), value.shape[0])
            weights[TALL][col.a, part, cols] = value.astype(BF16)

        for core in range(2):

            @pl.when(k == core)
            def _():
                top, bottom = (yw, xw) if core == 0 else (xw, yw)
                put(0, top[q, 0:off, :])
                row = lax.broadcasted_iota(jnp.int32, (8, quarter), 0)
                put(off, jnp.where(row < shift, top[q, off : off + 8, :], bottom[q, 0:8, :]))
                put(off + 8, bottom[q, 8:frame, :])

    order = [(0, 0), (0, 1), (1, 0), (0, 2), (1, 1), (0, 3), (1, 2), (1, 3)]
    order += [(i, j) for i in range(2, side) for j in range(side)]
    order = [(i, j) for i, j in order if i < side and j < side]
    left = [list(order), list(order)]

    def hand_on(p, count=1):
        for i, j in left[p][:count]:
            if i + j == 0:
                pl.semaphore_wait(ready.at[p], len(peers))
            each(4, lambda q, i=i, j=j: spread(p, i, j, q))
        del left[p][:count]

    tmp[...] = jnp.zeros_like(tmp)
    steps = [(s, j) for s in range(last) for j in range(side)]
    for s, j in steps:
        few(TALL, s, j)
    for at, (s, j) in enumerate(steps):
        if at % 2 == 0 and at // 2 < side:
            few(TALL, last, at // 2)
        few(WIDE, s, j)
        if at == 2 * last:
            each(4, lambda q: swap(q).start())
        if at == 2 * last + 1:
            let_in(TALL)
            for copy in loads:
                copy.wait()
            tall_step(0)
        if at == 2 * last + 2:
            tall_step(1)
        if at == 2 * last + 3:
            tall_step(2)
            tall_step(3)
        if at == 2 * last + 4:
            join(0)
            join(1)
        if at == 2 * last + 5:
            join(2)
            join(3)
    for j in range(side):
        few(WIDE, last, j)
        hand_on(TALL, 2 if j < last else 1)
    let_in(WIDE)
    for q in range(4):
        wide_step(q)
        hand_on(TALL)
    while left[WIDE] or left[TALL]:
        hand_on(WIDE)
        hand_on(TALL)
    for p in (TALL, WIDE):
        for q in range(4):
            wait_pieces(p, ring_send.at[p, q], chips - 1)
            wait_pieces(p, core_send.at[p, q], chips)
            wait_pieces(p, all_recv.at[p, q], chips)


def drain_kernel(count, *refs):
    sem = refs[-1]
    copies = []

    def copy(src, dst):
        copies.append(pltpu.make_async_copy(src, dst, sem.at[len(copies)]))

    at = count
    for here in refs[:count]:
        layers = 0
        while layers < here.shape[0]:
            there = refs[at]
            at += 1
            if there.shape == here.shape and there.shape[0] > 2:
                copy(here, there)
            else:
                size = there.shape[1] // PARTS
                size = size if size % 8 == 0 else there.shape[1]
                for a in range(there.shape[0]):
                    for b in range(0, there.shape[1], size):
                        copy(here.at[layers + a, pl.ds(b, size)], there.at[a, pl.ds(b, size)])
            layers += there.shape[0]
    for one in copies:
        one.start()
    for one in copies:
        one.wait()


def drain(arrays, like):
    return pl.pallas_call(
        functools.partial(drain_kernel, len(arrays)),
        out_shape=[jax.ShapeDtypeStruct(a.shape, a.dtype) for a in like],
        in_specs=[pl.BlockSpec(memory_space=pltpu.VMEM)] * len(arrays),
        out_specs=[pl.BlockSpec(memory_space=pl.ANY)] * len(like),
        scratch_shapes=[pltpu.SemaphoreType.DMA((2 * PARTS * len(like),))],
        compiler_params=pltpu.CompilerParams(vmem_limit_bytes=1 << 20),
    )(*arrays)


def solution(mesh):
    n = mesh.shape["dp"]

    def step(*arrays):
        g, w, m, v = (list(arrays[i : i + 3]) for i in (0, 3, 6, 9))
        m[2], v[2] = m[2].swapaxes(0, 1), v[2].swapaxes(0, 1)
        layers, rows, wide = m[0].shape
        low, _, narrow = m[2].shape
        side = math.isqrt(n // 2)
        quarter = narrow // 4
        frame = 2 * low - low // 8 * 8
        assert rows * wide == 4 * low * quarter and side * side * 2 == n and low % 8 and layers == 2
        dma, regular = pltpu.SemaphoreType.DMA, pltpu.SemaphoreType.REGULAR
        both = (2 * layers, *w[0].shape[1:])
        blocks = (2 * layers, rows, wide)
        outs = pl.pallas_call(
            functools.partial(step_kernel, n),
            out_shape=[
                pltpu.VMEM(both, BF16),
                pltpu.VMEM(w[2].shape, BF16),
                pltpu.VMEM(blocks, F32),
                pltpu.VMEM(m[2].shape, F32),
                pltpu.VMEM(blocks, F32),
                pltpu.VMEM(v[2].shape, F32),
            ],
            in_specs=[pl.BlockSpec(memory_space=pltpu.HBM)] * 12,
            out_specs=[pl.BlockSpec(memory_space=pltpu.VMEM)] * 6,
            scratch_shapes=[
                pltpu.VMEM((SLOTS, rows, wide), BF16),
                pltpu.VMEM((SLOTS, 2 * low, quarter), BF16),
                pltpu.VMEM(blocks, BF16),
                pltpu.VMEM((layers, frame, narrow), BF16),
                pltpu.VMEM((4, frame, quarter), BF16),
                pltpu.VMEM((4, frame, quarter), F32),
                pltpu.VMEM((4, frame, quarter), F32),
                pltpu.VMEM((4, frame, quarter), F32),
                pltpu.VMEM((frame, quarter), F32),
                dma((2, 4)),
                dma((2, 4, side * side)),
                dma((2, 4)),
                dma((2, 4 * side * side)),
                dma((2, 4)),
                dma((2, SLOTS)),
                dma((9,)),
                dma((4, 4)),
                regular((2,)),
            ],
            compiler_params=pltpu.CompilerParams(
                collective_id=0, has_side_effects=True, vmem_limit_bytes=14 << 20
            ),
        )(*g, *w, *m, *v)
        gate, up = drain(outs[:1], w[:2])
        down, *moments = drain(outs[1:], [w[2], *m, *v])
        for i in (2, 5):
            moments[i] = moments[i].swapaxes(0, 1)
        return gate, up, down, *moments

    all_of, cut = P(None, None, None), P(None, "dp", None)
    return jax.shard_map(
        step,
        mesh=mesh,
        in_specs=(P(("rep", "dp"), None, None, None),) * 3 + (all_of,) * 3 + (cut,) * 6,
        out_specs=(P("rep", None, None),) * 3 + (P("rep", "dp", None),) * 6,
        check_vma=False,
    )
```

time: 569 us -> 231 us (0.41)
  waiting for transfers between devices: 486 us -> 0 us
  Pallas kernels: 0 us -> 230 us
  local copies, waits for them, and re-layouts: 57 us -> 0 us
  between operations: 14.2 us -> 0.82 us
  other arithmetic: 11.1 us -> 0 us
    pallas_call x0 -> x3, Pallas kernels: none -> 230 us  [the longest x1 214 us: step(): pl.pallas_call(functools.partial(step_kernel, n), out_shape=[pltpu.VMEM(b...]
    reduce_scatter x2 -> x0, waiting for transfers between devices: 192 us -> none  [step(): lax.psum_scatter(t[0], 'dp', scatter_dimension=1, tiled=True)]
    all_gather x3 -> x0, waiting for transfers between devices: 168 us -> none  [step(): whole = [lax.all_gather(one[0], 'dp', axis=1, tiled=True) for one in new]]
    unnamed x7 -> x0, waiting for transfers between devices: 126 us -> none
    unnamed x12 -> x0, local copies, waits for them, and re-layouts: 55.9 us -> none
    convert_element_type x3 -> x0, other arithmetic: 11.1 us -> none  [adamw(): return ((w - 0.02 * step).astype(jnp.bfloat16), m, v)]
  transfers between devices with their start and end apart: 6 -> 0, of which waited for: 6 -> 0; matrix products, arithmetic and copies ran while one was open for 4% -> 0% of each run, Pallas kernels for 0% -> 0%
where the time goes in v4:
time: 231 us
  Pallas kernels  230 us (100%)
    pallas_call x1, Pallas kernels, step(): pl.pallas_call(functools.partial(step_kernel, n), out_shape=[pltpu.VMEM(b...  214 us
    pallas_call x2, Pallas kernels, drain(): pl.pallas_call(functools.partial(drain_kernel, len(arrays)), out_shape=[j...  16.2 us

profile of v4, /device:TPU:97, one launch (start us, length us, event | category | flops | bytes accessed | tf_op | source)
XLA Modules:
  0.0 230.7 jit_solution(3561530456296922227)
XLA Ops:
  0.6 213.7 %shard_map.187 = (bf16[4,1024,3200]{2,1,0:T(8,128)(2,1)S(1)}, bf16[2,3200,1024]{2,1,0:T(8,128)(2,1)S(1)}, f32[4,32,3200]{2,1,0:T(8,128)S(1)}, f32[100,2,1024]{2,...) custom-call(bf16[1,2,1024,3200]{3,2,1,0:T(8,128)(2,1)} %refs_0_.1, ...), custom_call_target="tpu_custom_call" | custom-call | tf_op jit(solution)/shard_map/pallas_call | solution.py:373
  214.3 9.0 %shard_map.188 = (bf16[2,1024,3200]{2,1,0:T(8,128)(2,1)}, bf16[2,1024,3200]{2,1,0:T(8,128)(2,1)}) custom-call(bf16[4,1024,3200]{2,1,0:T(8,128)(2,1)S(1)} %get-tuple-element.24.refs_0_), custom_call_target="tpu_custom_call" | custom-call | tf_op jit(solution)/shard_map/pallas_call | solution.py:348
  223.3 7.2 %shard_map.189 = (bf16[2,3200,1024]{2,1,0:T(8,128)(2,1)}, f32[2,32,3200]{2,1,0:T(8,128)}, f32[2,32,3200]{2,1,0:T(8,128)}, f32[100,2,1024]{2,1,0:T(2,128)}, f32[2...) custom-call(bf16[2,3200,1024]{2,1,0:T(8,128)(2,1)S(1)} %get-tuple-element.27.refs_0_, ...), custom_call_target="tpu_custom_call" | custom-call | tf_op jit(solution)/shard_map/pallas_call | solution.py:348

commit v5 on v4

--- a/solution.py
+++ b/solution.py
@@ -11,7 +11,7 @@
 MESH = pl.DeviceIdType.MESH
 F32, BF16 = jnp.float32, jnp.bfloat16
 SLOTS = 16
-PARTS = 8
+PARTS = 1
 WIDE, TALL = 0, 1
 
 
@@ -131,7 +131,6 @@
     each(SLOTS, functools.partial(load_own, TALL))
     pl.semaphore_wait(barrier, len(peers))
     each(ahead, functools.partial(to_partner, TALL))
-    each(SLOTS, functools.partial(load_own, WIDE))
 
     here = pl.ds(pl.multiple_of(me * rows, rows), rows)
     rim = pl.ds(pl.multiple_of(chip * tall + off * k, 8), frame)
@@ -140,9 +139,6 @@
         half = pl.ds(2 * a, 2)
         pairs += [(w[a].at[:, here], wsl.at[half]), (m[a], om.at[half]), (v[a], ov.at[half])]
     loads = [pltpu.make_async_copy(src, dst, in_sem.at[i]) for i, (src, dst) in enumerate(pairs)]
-    for copy in loads:
-        copy.start()
-
     def reduce(p, s, j, q):
         col = Colour(q)
         at = col.back(1 + s, 1 + j)
@@ -277,6 +273,10 @@
     steps = [(s, j) for s in range(last) for j in range(side)]
     for s, j in steps:
         few(TALL, s, j)
+        if (s, j) == (1, 0):
+            each(SLOTS, functools.partial(load_own, WIDE))
+            for copy in loads:
+                copy.start()
     for at, (s, j) in enumerate(steps):
         if at % 2 == 0 and at // 2 < side:
             few(TALL, last, at // 2)
@@ -300,8 +300,10 @@
             join(2)
             join(3)
     for j in range(side):
+        hand_on(TALL, 2 if j > 0 else 1)
         few(WIDE, last, j)
-        hand_on(TALL, 2 if j < last else 1)
+        if j == 0:
+            hand_on(TALL, 1)
     let_in(WIDE)
     for q in range(4):
         wide_step(q)

time: 231 us -> 230 us (level)
  no operation moved by 1% of the time
where the time goes in v5:
time: 230 us
  Pallas kernels  229 us (100%)
    pallas_call x1, Pallas kernels, step(): pl.pallas_call(functools.partial(step_kernel, n), out_shape=[pltpu.VMEM(b...  213 us
    pallas_call x2, Pallas kernels, drain(): pl.pallas_call(functools.partial(drain_kernel, len(arrays)), out_shape=[j...  15.3 us

profile of v5, /device:TPU:97, one launch (start us, length us, event | category | flops | bytes accessed | tf_op | source)
XLA Modules:
  0.0 229.6 jit_solution(14850043435468944596)
XLA Ops:
  0.6 213.5 %shard_map.187 = (bf16[4,1024,3200]{2,1,0:T(8,128)(2,1)S(1)}, bf16[2,3200,1024]{2,1,0:T(8,128)(2,1)S(1)}, f32[4,32,3200]{2,1,0:T(8,128)S(1)}, f32[100,2,1024]{2,...) custom-call(bf16[1,2,1024,3200]{3,2,1,0:T(8,128)(2,1)} %refs_0_.1, ...), custom_call_target="tpu_custom_call" | custom-call | tf_op jit(solution)/shard_map/pallas_call | solution.py:375
  214.1 8.9 %shard_map.188 = (bf16[2,1024,3200]{2,1,0:T(8,128)(2,1)}, bf16[2,1024,3200]{2,1,0:T(8,128)(2,1)}) custom-call(bf16[4,1024,3200]{2,1,0:T(8,128)(2,1)S(1)} %get-tuple-element.24.refs_0_), custom_call_target="tpu_custom_call" | custom-call | tf_op jit(solution)/shard_map/pallas_call | solution.py:350
  223.1 6.4 %shard_map.189 = (bf16[2,3200,1024]{2,1,0:T(8,128)(2,1)}, f32[2,32,3200]{2,1,0:T(8,128)}, f32[2,32,3200]{2,1,0:T(8,128)}, f32[100,2,1024]{2,1,0:T(2,128)}, f32[2...) custom-call(bf16[2,3200,1024]{2,1,0:T(8,128)(2,1)S(1)} %get-tuple-element.27.refs_0_, ...), custom_call_target="tpu_custom_call" | custom-call | tf_op jit(solution)/shard_map/pallas_call | solution.py:350

commit v6 on v5

--- a/solution.py
+++ b/solution.py
@@ -308,9 +308,11 @@
     for q in range(4):
         wide_step(q)
         hand_on(TALL)
-    while left[WIDE] or left[TALL]:
+    while left[WIDE]:
         hand_on(WIDE)
-        hand_on(TALL)
+        if len(left[TALL]) > side:
+            hand_on(TALL)
+    hand_on(TALL, len(left[TALL]))
     for p in (TALL, WIDE):
         for q in range(4):
             wait_pieces(p, ring_send.at[p, q], chips - 1)

time: 230 us -> 232 us (level)
    pallas_call x1, Pallas kernels: 213 us -> 216 us  [step(): pl.pallas_call(functools.partial(step_kernel, n), out_shape=[pltpu.VMEM(b...]
where the time goes in v6:
time: 232 us
  Pallas kernels  231 us (100%)
    pallas_call x1, Pallas kernels, step(): pl.pallas_call(functools.partial(step_kernel, n), out_shape=[pltpu.VMEM(b...  216 us
    pallas_call x2, Pallas kernels, drain(): pl.pallas_call(functools.partial(drain_kernel, len(arrays)), out_shape=[j...  15.3 us

profile of v6, /device:TPU:97, one launch (start us, length us, event | category | flops | bytes accessed | tf_op | source)
XLA Modules:
  0.0 232.0 jit_solution(16781603390393699961)
XLA Ops:
  0.6 215.9 %shard_map.187 = (bf16[4,1024,3200]{2,1,0:T(8,128)(2,1)S(1)}, bf16[2,3200,1024]{2,1,0:T(8,128)(2,1)S(1)}, f32[4,32,3200]{2,1,0:T(8,128)S(1)}, f32[100,2,1024]{2,...) custom-call(bf16[1,2,1024,3200]{3,2,1,0:T(8,128)(2,1)} %refs_0_.1, ...), custom_call_target="tpu_custom_call" | custom-call | tf_op jit(solution)/shard_map/pallas_call | solution.py:377
  216.5 8.9 %shard_map.188 = (bf16[2,1024,3200]{2,1,0:T(8,128)(2,1)}, bf16[2,1024,3200]{2,1,0:T(8,128)(2,1)}) custom-call(bf16[4,1024,3200]{2,1,0:T(8,128)(2,1)S(1)} %get-tuple-element.24.refs_0_), custom_call_target="tpu_custom_call" | custom-call | tf_op jit(solution)/shard_map/pallas_call | solution.py:352
  225.5 6.4 %shard_map.189 = (bf16[2,3200,1024]{2,1,0:T(8,128)(2,1)}, f32[2,32,3200]{2,1,0:T(8,128)}, f32[2,32,3200]{2,1,0:T(8,128)}, f32[100,2,1024]{2,1,0:T(2,128)}, f32[2...) custom-call(bf16[2,3200,1024]{2,1,0:T(8,128)(2,1)S(1)} %get-tuple-element.27.refs_0_, ...), custom_call_target="tpu_custom_call" | custom-call | tf_op jit(solution)/shard_map/pallas_call | solution.py:352
